TPU v7x, 32 devices: a whole 2x2x4 slice. The times are simulated.
32 devices in a mesh: region: 4 (over z), depth: 2 (over y), member: 4 (over x, core).
Axes of the slice: x: 2, y: 2, z: 4, core: 2. Of those that a mesh axis runs over, the one named last changes fastest.
Arguments:
- ensemble: bfloat16 [14, 384, 4096], P('depth', 'member', 'region'), may hold values from -6 to 6
- obs_weights: float32 [14], P('depth'), may hold values from -1.5 to 1.5
- obs_tiles: int32 [2048], P('region'), may hold values from 0 to 1023
- obs_values: float32 [2048], P('region'), may hold values from -8 to 8
- obs_error: float32 [2048], P('region'), may hold values from 0.2 to 2
- obs_noise: float32 [384, 2048], P('member', 'region'), may hold values from -6 to 6
Outputs:
- analysis: bfloat16 [14, 384, 4096], P('depth', 'member', 'region')
- inflation: float32 [], replicated
Inputs may be any that keep to these rules, and one draw needn't show every extreme that they name: `obs_tiles`: the tile of the observation, counted within the 1024 tiles of the region whose block holds the observation.
All inputs are finite; a program needn't handle non-finite values.
Results may differ from a plain program's by a relative error of at most 0.011.
Values may be sent and summed in bfloat16 or wider, within the bound.
A program may use at most 64 MiB of HBM per device.

v0:
```python
import jax
import jax.numpy as jnp
from jax import lax
from jax.sharding import PartitionSpec as P

MEMBERS = 384
RADIUS = 1024


def extended(array, sides, width):
    for axis, dim in sides:
        peers, length = (lax.axis_size(axis), array.shape[dim])
        up = [(i, (i + 1) % peers) for i in range(peers - 1)]
        down = [(j, i) for i, j in up]
        last = lax.slice_in_dim(array, length - width, length, axis=dim)
        leading = lax.slice_in_dim(array, 0, width, axis=dim)
        before = lax.ppermute(last, axis, up)
        after = lax.ppermute(leading, axis, down)
        array = jnp.concatenate([before, array, after], axis=dim)
    return array


def regress(
    anomalies, own_anom, state_mean, obs_anom, perturbed, factor, obs_pos, first_tile, infl_root
):
    var_count = anomalies.shape[0]
    tile_count = anomalies.shape[2]
    block = 128

    def one_block(block_index, output):
        block_start = block_index * block
        slab = lax.dynamic_slice_in_dim(anomalies, block_start, block, 2)
        own_slab = lax.dynamic_slice_in_dim(own_anom, block_start, block, 2)
        means = lax.dynamic_slice_in_dim(state_mean, block_start, block, 1)
        covariance = jnp.einsum(
            "lmt,mj->ltj", slab, obs_anom, preferred_element_type=jnp.float32
        ) / (MEMBERS - 1)
        tile_pos = (first_tile + block_start + jnp.arange(block, dtype=jnp.int32)).astype(
            jnp.float32
        )
        closeness = jnp.maximum(0.0, 1.0 - jnp.abs(tile_pos[:, None] - obs_pos[None, :]) / RADIUS)
        kalman_gain = (covariance * (closeness * closeness * factor[None, :])[None]).astype(
            jnp.bfloat16
        )
        increment = jnp.einsum(
            "ltj,mj->lmt", kalman_gain, perturbed, preferred_element_type=jnp.float32
        )
        updated = (means[:, None, :] + infl_root * own_slab.astype(jnp.float32) + increment).astype(
            jnp.bfloat16
        )
        return lax.dynamic_update_slice_in_dim(output, updated, block_start, 2)

    output = jnp.zeros((var_count, perturbed.shape[0], tile_count), jnp.bfloat16)
    return lax.fori_loop(0, tile_count // block, one_block, output)


def shards(ensemble, obs_weights, obs_tiles, obs_values, obs_error, obs_noise):
    tile_count = ensemble.shape[2]
    own_members = ensemble.shape[1]
    obs_count = obs_tiles.shape[0]
    member_sum = jnp.sum(ensemble, axis=1, dtype=jnp.float32)
    picked = jnp.take(ensemble, obs_tiles, axis=2).astype(jnp.float32)
    partial_pred = jnp.einsum("lmk,l->mk", picked, obs_weights, precision=lax.Precision.HIGHEST)
    predicted = lax.psum(partial_pred, "depth")
    totals = lax.psum(
        (member_sum, jnp.sum(predicted, axis=0), jnp.sum(predicted * predicted, axis=0)), "member"
    )
    state_mean = totals[0] / MEMBERS
    obs_mean = totals[1] / MEMBERS
    obs_dev = predicted - obs_mean[None, :]
    obs_spread = (totals[2] - MEMBERS * obs_mean * obs_mean) / (MEMBERS - 1)
    innovation = obs_values - obs_mean
    global_sums = lax.psum(
        (jnp.sum(innovation * innovation), jnp.sum(obs_spread + obs_error)), "region"
    )
    inflation = global_sums[0] / global_sums[1]
    infl_root = jnp.sqrt(inflation)
    factor = inflation / (inflation * obs_spread + obs_error)
    obs_anom = obs_dev.astype(jnp.bfloat16)
    perturbed = (
        innovation[None, :] + jnp.sqrt(obs_error)[None, :] * obs_noise - infl_root * obs_dev
    ).astype(jnp.bfloat16)
    first_tile = lax.axis_index("region") * tile_count
    obs_pos = (first_tile + obs_tiles).astype(jnp.float32)
    stacked = jnp.concatenate([obs_anom, perturbed], axis=0)
    widened = extended(stacked, (("region", 1),), obs_count)
    near_anom = widened[:own_members]
    near_pert = widened[own_members:]
    scalars = jnp.stack([factor, obs_pos], axis=0)
    wide_scalars = extended(scalars, (("region", 1),), obs_count)
    near_factor = wide_scalars[0]
    near_pos = wide_scalars[1]
    anomalies = (ensemble.astype(jnp.float32) - state_mean[:, None, :]).astype(jnp.bfloat16)
    all_anom, all_obs_anom = (
        lax.all_gather(anomalies, "member", axis=1, tiled=True),
        lax.all_gather(near_anom, "member", axis=0, tiled=True),
    )
    analysis = regress(
        all_anom,
        anomalies,
        state_mean,
        all_obs_anom,
        near_pert,
        near_factor,
        near_pos,
        first_tile,
        infl_root,
    )
    return (analysis, inflation)


def solution(mesh):
    return jax.shard_map(
        shards,
        mesh=mesh,
        in_specs=(
            P("depth", "member", "region"),
            P("depth"),
            P("region"),
            P("region"),
            P("region"),
            P("member", "region"),
        ),
        out_specs=(P("depth", "member", "region"), P()),
        check_vma=False,
    )
```

profile of v0, /device:TPU:0, one launch (start us, length us, event | category | flops | bytes accessed | tf_op | source)
XLA Modules:
  0.0 185.1 jit_solution(7628334277064460269)
XLA Ops:
  8.6 3.2 %copy.8 = bf16[7,96,1024]{1,0,2:T(8,128)(2,1)S(1)} copy(bf16[7,96,1024]{2,1,0:T(8,128)(2,1)} %param.8) | data formatting | bytes 2752512 | tf_op args[0]
  11.8 1.8 gather_fusion
  13.7 1.8 select_bitcast_fusion
  15.4 1.0 copy.9
  16.5 0.8 fusion.20
  17.3 0.7 copy.12
  18.4 25.0 %all-reduce.4.cloned.1.call-done = f32[96,512]{1,0:T(8,128)} async-done(((f32[96,512]{1,0:T(8,128)}), f32[96,512]{1,0:T(8,128)}) %all-reduce.4.cloned.1.call-update) | async-done | bytes 196624 | tf_op jit(solution)/shard_map/psum | solution.py:64
  43.3 1.0 multiply_reduce_fusion
  44.3 10.8 %all-reduce = (f32[7,1024]{1,0:T(8,128)S(1)}, f32[512]{0:T(512)S(1)}, f32[512]{0:T(512)S(1)}) all-reduce(f32[7,1024]{1,0:T(8,128)S(1)} %convert_reduce_fusion, f32[512]{0:T(512)S(1)} %get-tuple-element.188, f32[512]{0:T(512)S(1)} %get-tuple-element.187), channel_id=1, replica_groups=mesh['region'=4,'depth'=2,'member'=4] {'member'}, use_global_device_ids=true, to_apply=%region_1.2 | all-reduce | flops 8192 | bytes 65536 | tf_op jit(solution)/shard_map/psum | solution.py:65
  55.7 12.3 %all-reduce.1 = (f32[]{:T(128)}, f32[]{:T(128)}) all-reduce(f32[]{:T(128)} %get-tuple-element.216, f32[]{:T(128)} %get-tuple-element.229), channel_id=1, replica_groups=mesh['region'=4,'depth'=2,'member'=4] {'region'}, use_global_device_ids=true, to_apply=%region_6.7 | all-reduce | flops 2 | bytes 16 | tf_op jit(solution)/shard_map/psum | solution.py:73
  69.5 1.0 subtract_convert_fusion.1
  70.5 1.3 collective-permute-start.1
  71.8 4.6 %collective-permute-start = (bf16[192,512]{1,0:T(8,128)(2,1)S(1)}, bf16[192,512]{1,0:T(8,128)(2,1)S(1)}, u32[]{:S(2)}, u32[]{:S(2)}) collective-permute-start(bf16[192,512]{1,0:T(8,128)(2,1)S(1)} %pad_maximum_fusion.1), channel_id=1, source_target_pairs={{0,8},{8,16},{16,24},{1,9},{9,17},{17,25},{2,10},{10,18},{18,26},{... | collective-permute-start | bytes 589832 | tf_op jit(solution)/shard_map/ppermute | solution.py:17
  76.4 1.7 collective-permute-done.1
  78.1 1.5 collective-permute-done
  79.6 0.8 fusion.23
  80.4 1.4 fusion.18
  81.9 1.3 collective-permute-start.3
  83.2 5.0 %collective-permute-start.2 = (f32[2,512]{1,0:T(2,128)S(1)}, f32[2,512]{1,0:T(2,128)S(1)}, u32[]{:S(2)}, u32[]{:S(2)}) collective-permute-start(f32[2,512]{1,0:T(2,128)S(1)} %pad_maximum_fusion.3), channel_id=1, source_target_pairs={{0,8},{8,16},{16,24},{1,9},{9,17},{17,25},{2,10},{10,18},{18,26},{... | collective-permute-start | bytes 12296 | tf_op jit(solution)/shard_map/ppermute | solution.py:17
  88.2 1.3 collective-permute-done.2
  89.6 7.4 %all-gather.5.cloned.1.call-done = bf16[384,1536]{1,0:T(8,128)(2,1)} async-done(((bf16[96,1536]{1,0:T(8,128)(2,1)}), bf16[384,1536]{1,0:T(8,128)(2,1)}) %all-gather.5.cloned.1.call-update) | async-done | bytes 1179664 | tf_op jit(solution)/shard_map/all_gather | solution.py:96
  97.0 44.1 %all-gather.3.cloned.1.call-done = bf16[7,384,1024]{2,1,0:T(8,128)(2,1)} async-done(((bf16[7,96,1024]{2,1,0:T(8,128)(2,1)}), bf16[7,384,1024]{2,1,0:T(8,128)(2,1)}) %all-gather.3.cloned.1.call-update) | async-done | bytes 5505040 | tf_op jit(solution)/shard_map/all_gather | solution.py:95
  141.2 35.1 %while.13 = (s32[]{:T(128)}, bf16[7,96,1024]{2,1,0:T(8,128)(2,1)S(1)}, f32[7,1024]{1,0:T(8,128)S(1)}, f32[]{:T(128)}, bf16[7,96,1024]{2,1,0:T(8,128)(2,1)}, /*in...) while((s32[]{:T(128)}, ...), condition=%wide.region_12.13_spmd, body=%wide.region_11.12_spmd.sunk | while | flops 1325961472 | bytes 4130527 | solution.py:54
  141.6 4.0 %fusion.33 = bf16[7,96,1024]{2,1,0:T(8,128)(2,1)S(1)} fusion(bf16[7,96,1024]{2,1,0:T(8,128)(2,1)S(1)} %get-tuple-element.314, s32[]{:T(128)S(6)} %select_n.27, f32[128,1536]{1,0:T(8,128)S(1)} %multiply_multiply_fusion.2, bf16[384,1536]{1,0:T(8,128)(2,1)} %get-tuple-element.335, bf16[7,384,1024]{2,1,0:T(8,128)(2,1)} %get-tuple-element.334, ...), kind=kOutput, calls=%fused_computation.7.clone.1 | convolution fusion | flops 1324388352 | bytes 3298816 | tf_op jit(solution)/shard_map/while/body/eval_jaxpr/ltj,mj->lmt/dot_general | solution.py:45
  146.0 4.0 %fusion.33 = bf16[7,96,1024]{2,1,0:T(8,128)(2,1)S(1)} fusion(bf16[7,96,1024]{2,1,0:T(8,128)(2,1)S(1)} %get-tuple-element.314, s32[]{:T(128)S(6)} %select_n.27, f32[128,1536]{1,0:T(8,128)S(1)} %multiply_multiply_fusion.2, bf16[384,1536]{1,0:T(8,128)(2,1)} %get-tuple-element.335, bf16[7,384,1024]{2,1,0:T(8,128)(2,1)} %get-tuple-element.334, ...), kind=kOutput, calls=%fused_computation.7.clone.1 | convolution fusion | flops 1324388352 | bytes 3298816 | tf_op jit(solution)/shard_map/while/body/eval_jaxpr/ltj,mj->lmt/dot_general | solution.py:45
  150.4 4.0 %fusion.33 = bf16[7,96,1024]{2,1,0:T(8,128)(2,1)S(1)} fusion(bf16[7,96,1024]{2,1,0:T(8,128)(2,1)S(1)} %get-tuple-element.314, s32[]{:T(128)S(6)} %select_n.27, f32[128,1536]{1,0:T(8,128)S(1)} %multiply_multiply_fusion.2, bf16[384,1536]{1,0:T(8,128)(2,1)} %get-tuple-element.335, bf16[7,384,1024]{2,1,0:T(8,128)(2,1)} %get-tuple-element.334, ...), kind=kOutput, calls=%fused_computation.7.clone.1 | convolution fusion | flops 1324388352 | bytes 3298816 | tf_op jit(solution)/shard_map/while/body/eval_jaxpr/ltj,mj->lmt/dot_general | solution.py:45
  154.8 4.0 %fusion.33 = bf16[7,96,1024]{2,1,0:T(8,128)(2,1)S(1)} fusion(bf16[7,96,1024]{2,1,0:T(8,128)(2,1)S(1)} %get-tuple-element.314, s32[]{:T(128)S(6)} %select_n.27, f32[128,1536]{1,0:T(8,128)S(1)} %multiply_multiply_fusion.2, bf16[384,1536]{1,0:T(8,128)(2,1)} %get-tuple-element.335, bf16[7,384,1024]{2,1,0:T(8,128)(2,1)} %get-tuple-element.334, ...), kind=kOutput, calls=%fused_computation.7.clone.1 | convolution fusion | flops 1324388352 | bytes 3298816 | tf_op jit(solution)/shard_map/while/body/eval_jaxpr/ltj,mj->lmt/dot_general | solution.py:45
  159.2 4.0 %fusion.33 = bf16[7,96,1024]{2,1,0:T(8,128)(2,1)S(1)} fusion(bf16[7,96,1024]{2,1,0:T(8,128)(2,1)S(1)} %get-tuple-element.314, s32[]{:T(128)S(6)} %select_n.27, f32[128,1536]{1,0:T(8,128)S(1)} %multiply_multiply_fusion.2, bf16[384,1536]{1,0:T(8,128)(2,1)} %get-tuple-element.335, bf16[7,384,1024]{2,1,0:T(8,128)(2,1)} %get-tuple-element.334, ...), kind=kOutput, calls=%fused_computation.7.clone.1 | convolution fusion | flops 1324388352 | bytes 3298816 | tf_op jit(solution)/shard_map/while/body/eval_jaxpr/ltj,mj->lmt/dot_general | solution.py:45
  163.6 4.0 %fusion.33 = bf16[7,96,1024]{2,1,0:T(8,128)(2,1)S(1)} fusion(bf16[7,96,1024]{2,1,0:T(8,128)(2,1)S(1)} %get-tuple-element.314, s32[]{:T(128)S(6)} %select_n.27, f32[128,1536]{1,0:T(8,128)S(1)} %multiply_multiply_fusion.2, bf16[384,1536]{1,0:T(8,128)(2,1)} %get-tuple-element.335, bf16[7,384,1024]{2,1,0:T(8,128)(2,1)} %get-tuple-element.334, ...), kind=kOutput, calls=%fused_computation.7.clone.1 | convolution fusion | flops 1324388352 | bytes 3298816 | tf_op jit(solution)/shard_map/while/body/eval_jaxpr/ltj,mj->lmt/dot_general | solution.py:45
  167.9 4.0 %fusion.33 = bf16[7,96,1024]{2,1,0:T(8,128)(2,1)S(1)} fusion(bf16[7,96,1024]{2,1,0:T(8,128)(2,1)S(1)} %get-tuple-element.314, s32[]{:T(128)S(6)} %select_n.27, f32[128,1536]{1,0:T(8,128)S(1)} %multiply_multiply_fusion.2, bf16[384,1536]{1,0:T(8,128)(2,1)} %get-tuple-element.335, bf16[7,384,1024]{2,1,0:T(8,128)(2,1)} %get-tuple-element.334, ...), kind=kOutput, calls=%fused_computation.7.clone.1 | convolution fusion | flops 1324388352 | bytes 3298816 | tf_op jit(solution)/shard_map/while/body/eval_jaxpr/ltj,mj->lmt/dot_general | solution.py:45
  172.3 4.0 %fusion.33 = bf16[7,96,1024]{2,1,0:T(8,128)(2,1)S(1)} fusion(bf16[7,96,1024]{2,1,0:T(8,128)(2,1)S(1)} %get-tuple-element.314, s32[]{:T(128)S(6)} %select_n.27, f32[128,1536]{1,0:T(8,128)S(1)} %multiply_multiply_fusion.2, bf16[384,1536]{1,0:T(8,128)(2,1)} %get-tuple-element.335, bf16[7,384,1024]{2,1,0:T(8,128)(2,1)} %get-tuple-element.334, ...), kind=kOutput, calls=%fused_computation.7.clone.1 | convolution fusion | flops 1324388352 | bytes 3298816 | tf_op jit(solution)/shard_map/while/body/eval_jaxpr/ltj,mj->lmt/dot_general | solution.py:45
  176.4 1.1 copy-done.2
  (71 shorter events, 5.4 us)
Async XLA Ops:
  7.2 9.3 %copy-start = (f32[7]{0:T(128)S(1)}, f32[7]{0:T(128)}, u32[]{:S(2)}) copy-start(f32[7]{0:T(128)} %param.9) | copy-start | bytes 88
  7.2 36.1 %all-reduce.4.cloned.1.call-start = ((), (), s32[]{:S(2)}) async-start(), calls=%async_computation | async-start | bytes 393216 | tf_op jit(solution)/shard_map/psum | solution.py:64
  15.4 2.6 %copy-start.1 = (bf16[7,96,1024]{2,1,0:T(8,128)(2,1)S(1)}, bf16[7,96,1024]{2,1,0:T(8,128)(2,1)}, u32[]{:S(2)}) copy-start(bf16[7,96,1024]{2,1,0:T(8,128)(2,1)} %param.8) | copy-start | bytes 4128772
  16.5 38.6 %copy-start.4 = (f32[512]{0:T(512)S(1)}, f32[512]{0:T(512)}, u32[]{:S(2)}) copy-start(f32[512]{0:T(512)} %param.12) | copy-start | bytes 6148
  16.5 38.6 %copy-start.5 = (f32[512]{0:T(512)S(1)}, f32[512]{0:T(512)}, u32[]{:S(2)}) copy-start(f32[512]{0:T(512)} %param.11) | copy-start | bytes 6148
  17.3 52.2 %copy-start.3 = (f32[96,512]{1,0:T(8,128)S(1)}, f32[96,512]{1,0:T(8,128)}, u32[]{:S(2)}) copy-start(f32[96,512]{1,0:T(8,128)} %param.13) | copy-start | bytes 589828
  18.0 79.0 %all-gather.5.cloned.1.call-start = ((), (), s32[]{:S(2)}) async-start(), calls=%async_computation.2 | async-start | bytes 1474560 | tf_op jit(solution)/shard_map/all_gather | solution.py:96
  70.5 7.6 %collective-permute-start.1 = (bf16[192,512]{1,0:T(8,128)(2,1)S(1)}, bf16[192,512]{1,0:T(8,128)(2,1)S(1)}, u32[]{:S(2)}, u32[]{:S(2)}) collective-permute-start(bf16[192,512]{1,0:T(8,128)(2,1)S(1)} %pad_maximum_fusion.1), channel_id=1, source_target_pairs={{8,0},{16,8},{24,16},{9,1},{17,9},{25,17},{10,2},{18,10},{26,18},{... | collective-permute-start | bytes 589832 | tf_op jit(solution)/shard_map/ppermute | solution.py:18
  71.8 7.7 %collective-permute-start = (bf16[192,512]{1,0:T(8,128)(2,1)S(1)}, bf16[192,512]{1,0:T(8,128)(2,1)S(1)}, u32[]{:S(2)}, u32[]{:S(2)}) collective-permute-start(bf16[192,512]{1,0:T(8,128)(2,1)S(1)} %pad_maximum_fusion.1), channel_id=1, source_target_pairs={{0,8},{8,16},{16,24},{1,9},{9,17},{17,25},{2,10},{10,18},{18,26},{... | collective-permute-start | bytes 589832 | tf_op jit(solution)/shard_map/ppermute | solution.py:17
  80.4 60.7 %all-gather.3.cloned.1.call-start = ((), (), s32[]{:S(2)}) async-start(), calls=%async_computation.1 | async-start | bytes 6881280 | tf_op jit(solution)/shard_map/all_gather | solution.py:95
  81.9 6.3 %collective-permute-start.3 = (f32[2,512]{1,0:T(2,128)S(1)}, f32[2,512]{1,0:T(2,128)S(1)}, u32[]{:S(2)}, u32[]{:S(2)}) collective-permute-start(f32[2,512]{1,0:T(2,128)S(1)} %pad_maximum_fusion.3), channel_id=1, source_target_pairs={{8,0},{16,8},{24,16},{9,1},{17,9},{25,17},{10,2},{18,10},{26,18},{... | collective-permute-start | bytes 12296 | tf_op jit(solution)/shard_map/ppermute | solution.py:18
  83.2 6.3 %collective-permute-start.2 = (f32[2,512]{1,0:T(2,128)S(1)}, f32[2,512]{1,0:T(2,128)S(1)}, u32[]{:S(2)}, u32[]{:S(2)}) collective-permute-start(f32[2,512]{1,0:T(2,128)S(1)} %pad_maximum_fusion.3), channel_id=1, source_target_pairs={{0,8},{8,16},{16,24},{1,9},{9,17},{17,25},{2,10},{10,18},{18,26},{... | collective-permute-start | bytes 12296 | tf_op jit(solution)/shard_map/ppermute | solution.py:17
  176.3 1.1 copy-start.2
Sparse Core Ops, SparseCore 0:
  18.1 25.1 all-reduce.3
  80.5 16.4 all-gather.4
  99.1 41.8 all-gather.2
where the time goes:
time: 186 us; the launch traced here: 185 us
  waiting for transfers between devices  80.9 us (43%)
  matrix products  32.7 us (18%)
  blocking collectives  23.2 us (12%)
  between operations  16.5 us (9%)
  starting transfers between devices  12.3 us (7%)
  other arithmetic  10.1 us (5%)
  local copies, waits for them, and re-layouts  8.89 us (5%)
    all_gather x1, waiting for transfers between devices, shards(): lax.all_gather(anomalies, 'member', axis=1, tiled=True)  44.1 us
    dot_general x8, matrix products, one_block(): jnp.einsum('ltj,mj->lmt', kalman_gain, perturbed, preferred_element_type=...  31.9 us
    psum x1, waiting for transfers between devices, shards(): predicted = lax.psum(partial_pred, 'depth')  25 us
    psum x1, blocking collectives, shards(): lax.psum((jnp.sum(innovation * innovation), jnp.sum(obs_spread + obs_erro...  12.3 us
    psum x1, blocking collectives, shards(): lax.psum((member_sum, jnp.sum(predicted, axis=0), jnp.sum(predicted * pre...  10.8 us
    ppermute x2, starting transfers between devices, extended(): before = lax.ppermute(last, axis, up)  9.57 us
    all_gather x1, waiting for transfers between devices, shards(): lax.all_gather(near_anom, 'member', axis=0, tiled=True)  7.4 us
    unnamed x13, local copies, waits for them, and re-layouts  4.34 us
  transfers between devices with their start and end apart: 7, of which 6 were waited for; matrix products, arithmetic and copies ran while one was open for 1% of the time, Pallas kernels for 0%

commit v1 on v0

--- a/solution.py
+++ b/solution.py
@@ -61,7 +61,7 @@
     member_sum = jnp.sum(ensemble, axis=1, dtype=jnp.float32)
     picked = jnp.take(ensemble, obs_tiles, axis=2).astype(jnp.float32)
     partial_pred = jnp.einsum("lmk,l->mk", picked, obs_weights, precision=lax.Precision.HIGHEST)
-    predicted = lax.psum(partial_pred, "depth")
+    predicted = jnp.sum(lax.all_gather(partial_pred, "depth"), axis=0)
     totals = lax.psum(
         (member_sum, jnp.sum(predicted, axis=0), jnp.sum(predicted * predicted, axis=0)), "member"
     )

time: 186 us -> 169 us (0.909)
  waiting for transfers between devices: 80.9 us -> 57.3 us
  blocking collectives: 23.2 us -> 31.8 us
    psum x1 -> x0, waiting for transfers between devices: 25 us -> none  [shards(): predicted = lax.psum(partial_pred, 'depth')]
    all_gather x0 -> x1, blocking collectives: none -> 8.56 us  [shards(): predicted = jnp.sum(lax.all_gather(partial_pred, 'depth'), axis=0)]
    unnamed x13 -> x15, local copies, waits for them, and re-layouts: 4.34 us -> 3.25 us
  transfers between devices with their start and end apart: 7 -> 6, of which waited for: 6 -> 5; matrix products, arithmetic and copies ran while one was open for 1% -> 1% of each run, Pallas kernels for 0% -> 0%
where the time goes in v1:
time: 169 us
  waiting for transfers between devices  57.3 us (34%)
  matrix products  32.6 us (19%)
  blocking collectives  31.8 us (19%)
  between operations  16.8 us (10%)
  starting transfers between devices  12.2 us (7%)
  other arithmetic  9.73 us (6%)
  local copies, waits for them, and re-layouts  7.7 us (5%)
    all_gather x1, waiting for transfers between devices, shards(): lax.all_gather(anomalies, 'member', axis=1, tiled=True)  44.1 us
    dot_general x8, matrix products, one_block(): jnp.einsum('ltj,mj->lmt', kalman_gain, perturbed, preferred_element_type=...  31.8 us
    psum x1, blocking collectives, shards(): lax.psum((jnp.sum(innovation * innovation), jnp.sum(obs_spread + obs_erro...  12.6 us
    psum x1, blocking collectives, shards(): lax.psum((member_sum, jnp.sum(predicted, axis=0), jnp.sum(predicted * pre...  10.7 us
    ppermute x2, starting transfers between devices, extended(): before = lax.ppermute(last, axis, up)  9.57 us
    all_gather x1, waiting for transfers between devices, shards(): lax.all_gather(near_anom, 'member', axis=0, tiled=True)  8.7 us
    all_gather x1, blocking collectives, shards(): predicted = jnp.sum(lax.all_gather(partial_pred, 'depth'), axis=0)  8.56 us
  transfers between devices with their start and end apart: 6, of which 5 were waited for; matrix products, arithmetic and copies ran while one was open for 1% of the time, Pallas kernels for 0%

profile of v1, /device:TPU:0, one launch (start us, length us, event | category | flops | bytes accessed | tf_op | source)
XLA Modules:
  0.0 168.7 jit_solution(17583082966844297893)
XLA Ops:
  7.2 1.7 %convert_reduce_fusion = f32[7,1024]{1,0:T(8,128)S(1)} fusion(bf16[7,96,1024]{2,1,0:T(8,128)(2,1)} %param.8), kind=kLoop, calls=%fused_computation.15 | loop fusion | flops 1369088 | bytes 1404928 | tf_op jit(solution)/shard_map/reduce_sum | solution.py:61
  9.0 2.1 %copy.11 = bf16[7,96,1024]{1,0,2:T(8,128)(2,1)S(1)} copy(bf16[7,96,1024]{2,1,0:T(8,128)(2,1)S(1)} %copy-done.1) | data formatting | bytes 2752512 | tf_op args[0]
  11.2 2.4 %gather_fusion = bf16[512,7,96]{2,1,0:T(8,128)(2,1)} fusion(bf16[7,96,1024]{1,0,2:T(8,128)(2,1)S(1)} %copy.11, s32[1024]{0:T(1024)S(1)} %pad_clamp_fusion), kind=kCustom, calls=%fused_computation | custom fusion | bytes 1378304 | tf_op jit(solution)/shard_map/jit(_take)/gather | solution.py:62
  13.6 3.1 %select_bitcast_fusion = bf16[7,96,512]{1,0,2:T(8,128)(2,1)S(1)} fusion(bf16[512,7,96]{2,1,0:T(8,128)(2,1)} %gather_fusion, pred[512]{0:T(512)(128)(4,1)S(1)} %compare_and_fusion), kind=kLoop, calls=%fused_computation.17 | loop fusion | flops 344064 | bytes 1376768 | tf_op jit(solution)/shard_map/jit(_take)/select_n | solution.py:62
  16.7 1.0 copy.13
  17.8 0.8 fusion.20
  18.6 8.6 %all-gather = f32[192,512]{1,0:T(8,128)S(1)} all-gather(f32[96,512]{1,0:T(8,128)S(1)} %bitcast.40), channel_id=2, replica_groups=mesh['region'=4,'depth'=2,'member'=4] {'depth'}, dimensions={0}, use_global_device_ids=true | all-gather | bytes 589824 | tf_op jit(solution)/shard_map/all_gather | solution.py:64
  27.2 10.7 %all-reduce = (f32[7,1024]{1,0:T(8,128)S(1)}, f32[512]{0:T(512)S(1)}, f32[512]{0:T(512)S(1)}) all-reduce(f32[7,1024]{1,0:T(8,128)S(1)} %convert_reduce_fusion, f32[512]{0:T(512)S(1)} %reduce_sum.55, f32[512]{0:T(512)S(1)} %multiply_reduce_fusion), channel_id=1, replica_groups=mesh['region'=4,'depth'=2,'member'=4] {'member'}, use_global_device_ids=true, to_apply=%region_1.2 | all-reduce | flops 8192 | bytes 65536 | tf_op jit(solution)/shard_map/psum | solution.py:65
  38.0 0.6 multiply_reduce_fusion.1
  38.6 12.6 %all-reduce.1 = (f32[]{:T(128)}, f32[]{:T(128)}) all-reduce(f32[]{:T(128)} %get-tuple-element.225, f32[]{:T(128)} %get-tuple-element.238), channel_id=1, replica_groups=mesh['region'=4,'depth'=2,'member'=4] {'region'}, use_global_device_ids=true, to_apply=%region_6.7 | all-reduce | flops 2 | bytes 16 | tf_op jit(solution)/shard_map/psum | solution.py:73
  52.7 1.3 collective-permute-start.1
  54.0 4.6 %collective-permute-start = (bf16[192,512]{1,0:T(8,128)(2,1)S(1)}, bf16[192,512]{1,0:T(8,128)(2,1)S(1)}, u32[]{:S(2)}, u32[]{:S(2)}) collective-permute-start(bf16[192,512]{1,0:T(8,128)(2,1)S(1)} %pad_maximum_fusion.1), channel_id=1, source_target_pairs={{0,8},{8,16},{16,24},{1,9},{9,17},{17,25},{2,10},{10,18},{18,26},{... | collective-permute-start | bytes 589832 | tf_op jit(solution)/shard_map/ppermute | solution.py:17
  58.5 1.7 %collective-permute-done.1 = bf16[192,512]{1,0:T(8,128)(2,1)S(1)} collective-permute-done((bf16[192,512]{1,0:T(8,128)(2,1)S(1)}, bf16[192,512]{1,0:T(8,128)(2,1)S(1)}, u32[]{:S(2)}, u32[]{:S(2)}) %collective-permute-start.1) | collective-permute-done | bytes 196640 | tf_op jit(solution)/shard_map/ppermute | solution.py:18
  60.2 1.5 collective-permute-done
  61.7 0.8 fusion.23
  62.6 1.4 fusion.18
  64.1 1.3 collective-permute-start.3
  65.4 5.0 %collective-permute-start.2 = (f32[2,512]{1,0:T(2,128)S(1)}, f32[2,512]{1,0:T(2,128)S(1)}, u32[]{:S(2)}, u32[]{:S(2)}) collective-permute-start(f32[2,512]{1,0:T(2,128)S(1)} %pad_maximum_fusion.3), channel_id=1, source_target_pairs={{0,8},{8,16},{16,24},{1,9},{9,17},{17,25},{2,10},{10,18},{18,26},{... | collective-permute-start | bytes 12296 | tf_op jit(solution)/shard_map/ppermute | solution.py:17
  70.4 1.3 collective-permute-done.2
  71.7 8.7 %all-gather.6.cloned.1.call-done = bf16[384,1536]{1,0:T(8,128)(2,1)} async-done(((bf16[96,1536]{1,0:T(8,128)(2,1)}), bf16[384,1536]{1,0:T(8,128)(2,1)}) %all-gather.6.cloned.1.call-update) | async-done | bytes 1179664 | tf_op jit(solution)/shard_map/all_gather | solution.py:96
  80.4 44.1 %all-gather.4.cloned.1.call-done = bf16[7,384,1024]{2,1,0:T(8,128)(2,1)} async-done(((bf16[7,96,1024]{2,1,0:T(8,128)(2,1)}), bf16[7,384,1024]{2,1,0:T(8,128)(2,1)}) %all-gather.4.cloned.1.call-update) | async-done | bytes 5505040 | tf_op jit(solution)/shard_map/all_gather | solution.py:95
  124.7 35.0 %while.13 = (s32[]{:T(128)}, bf16[7,96,1024]{2,1,0:T(8,128)(2,1)S(1)}, f32[7,1024]{1,0:T(8,128)S(1)}, f32[]{:T(128)}, bf16[7,96,1024]{2,1,0:T(8,128)(2,1)}, /*in...) while((s32[]{:T(128)}, ...), condition=%wide.region_12.13_spmd, body=%wide.region_11.12_spmd.sunk | while | flops 1325961472 | bytes 4130527 | solution.py:54
  124.8 0.3 multiply_multiply_fusion.2
  125.0 4.0 %fusion.33 = bf16[7,96,1024]{2,1,0:T(8,128)(2,1)S(1)} fusion(bf16[7,96,1024]{2,1,0:T(8,128)(2,1)S(1)} %get-tuple-element.323, s32[]{:T(128)S(6)} %select_n.27, f32[128,1536]{1,0:T(8,128)S(1)} %multiply_multiply_fusion.2, bf16[384,1536]{1,0:T(8,128)(2,1)} %get-tuple-element.344, bf16[7,384,1024]{2,1,0:T(8,128)(2,1)} %get-tuple-element.343, ...), kind=kOutput, calls=%fused_computation.7.clone.1 | convolution fusion | flops 1324388352 | bytes 3298816 | tf_op jit(solution)/shard_map/while/body/eval_jaxpr/ltj,mj->lmt/dot_general | solution.py:45
  129.4 4.0 %fusion.33 = bf16[7,96,1024]{2,1,0:T(8,128)(2,1)S(1)} fusion(bf16[7,96,1024]{2,1,0:T(8,128)(2,1)S(1)} %get-tuple-element.323, s32[]{:T(128)S(6)} %select_n.27, f32[128,1536]{1,0:T(8,128)S(1)} %multiply_multiply_fusion.2, bf16[384,1536]{1,0:T(8,128)(2,1)} %get-tuple-element.344, bf16[7,384,1024]{2,1,0:T(8,128)(2,1)} %get-tuple-element.343, ...), kind=kOutput, calls=%fused_computation.7.clone.1 | convolution fusion | flops 1324388352 | bytes 3298816 | tf_op jit(solution)/shard_map/while/body/eval_jaxpr/ltj,mj->lmt/dot_general | solution.py:45
  133.8 4.0 %fusion.33 = bf16[7,96,1024]{2,1,0:T(8,128)(2,1)S(1)} fusion(bf16[7,96,1024]{2,1,0:T(8,128)(2,1)S(1)} %get-tuple-element.323, s32[]{:T(128)S(6)} %select_n.27, f32[128,1536]{1,0:T(8,128)S(1)} %multiply_multiply_fusion.2, bf16[384,1536]{1,0:T(8,128)(2,1)} %get-tuple-element.344, bf16[7,384,1024]{2,1,0:T(8,128)(2,1)} %get-tuple-element.343, ...), kind=kOutput, calls=%fused_computation.7.clone.1 | convolution fusion | flops 1324388352 | bytes 3298816 | tf_op jit(solution)/shard_map/while/body/eval_jaxpr/ltj,mj->lmt/dot_general | solution.py:45
  138.2 4.0 %fusion.33 = bf16[7,96,1024]{2,1,0:T(8,128)(2,1)S(1)} fusion(bf16[7,96,1024]{2,1,0:T(8,128)(2,1)S(1)} %get-tuple-element.323, s32[]{:T(128)S(6)} %select_n.27, f32[128,1536]{1,0:T(8,128)S(1)} %multiply_multiply_fusion.2, bf16[384,1536]{1,0:T(8,128)(2,1)} %get-tuple-element.344, bf16[7,384,1024]{2,1,0:T(8,128)(2,1)} %get-tuple-element.343, ...), kind=kOutput, calls=%fused_computation.7.clone.1 | convolution fusion | flops 1324388352 | bytes 3298816 | tf_op jit(solution)/shard_map/while/body/eval_jaxpr/ltj,mj->lmt/dot_general | solution.py:45
  142.5 4.0 %fusion.33 = bf16[7,96,1024]{2,1,0:T(8,128)(2,1)S(1)} fusion(bf16[7,96,1024]{2,1,0:T(8,128)(2,1)S(1)} %get-tuple-element.323, s32[]{:T(128)S(6)} %select_n.27, f32[128,1536]{1,0:T(8,128)S(1)} %multiply_multiply_fusion.2, bf16[384,1536]{1,0:T(8,128)(2,1)} %get-tuple-element.344, bf16[7,384,1024]{2,1,0:T(8,128)(2,1)} %get-tuple-element.343, ...), kind=kOutput, calls=%fused_computation.7.clone.1 | convolution fusion | flops 1324388352 | bytes 3298816 | tf_op jit(solution)/shard_map/while/body/eval_jaxpr/ltj,mj->lmt/dot_general | solution.py:45
  146.9 4.0 %fusion.33 = bf16[7,96,1024]{2,1,0:T(8,128)(2,1)S(1)} fusion(bf16[7,96,1024]{2,1,0:T(8,128)(2,1)S(1)} %get-tuple-element.323, s32[]{:T(128)S(6)} %select_n.27, f32[128,1536]{1,0:T(8,128)S(1)} %multiply_multiply_fusion.2, bf16[384,1536]{1,0:T(8,128)(2,1)} %get-tuple-element.344, bf16[7,384,1024]{2,1,0:T(8,128)(2,1)} %get-tuple-element.343, ...), kind=kOutput, calls=%fused_computation.7.clone.1 | convolution fusion | flops 1324388352 | bytes 3298816 | tf_op jit(solution)/shard_map/while/body/eval_jaxpr/ltj,mj->lmt/dot_general | solution.py:45
  151.3 4.0 %fusion.33 = bf16[7,96,1024]{2,1,0:T(8,128)(2,1)S(1)} fusion(bf16[7,96,1024]{2,1,0:T(8,128)(2,1)S(1)} %get-tuple-element.323, s32[]{:T(128)S(6)} %select_n.27, f32[128,1536]{1,0:T(8,128)S(1)} %multiply_multiply_fusion.2, bf16[384,1536]{1,0:T(8,128)(2,1)} %get-tuple-element.344, bf16[7,384,1024]{2,1,0:T(8,128)(2,1)} %get-tuple-element.343, ...), kind=kOutput, calls=%fused_computation.7.clone.1 | convolution fusion | flops 1324388352 | bytes 3298816 | tf_op jit(solution)/shard_map/while/body/eval_jaxpr/ltj,mj->lmt/dot_general | solution.py:45
  155.6 4.0 %fusion.33 = bf16[7,96,1024]{2,1,0:T(8,128)(2,1)S(1)} fusion(bf16[7,96,1024]{2,1,0:T(8,128)(2,1)S(1)} %get-tuple-element.323, s32[]{:T(128)S(6)} %select_n.27, f32[128,1536]{1,0:T(8,128)S(1)} %multiply_multiply_fusion.2, bf16[384,1536]{1,0:T(8,128)(2,1)} %get-tuple-element.344, bf16[7,384,1024]{2,1,0:T(8,128)(2,1)} %get-tuple-element.343, ...), kind=kOutput, calls=%fused_computation.7.clone.1 | convolution fusion | flops 1324388352 | bytes 3298816 | tf_op jit(solution)/shard_map/while/body/eval_jaxpr/ltj,mj->lmt/dot_general | solution.py:45
  159.6 1.1 copy-done.2
  (73 shorter events, 3.0 us)
Async XLA Ops:
  7.2 10.6 %copy-start = (f32[7]{0:T(128)S(1)}, f32[7]{0:T(128)}, u32[]{:S(2)}) copy-start(f32[7]{0:T(128)} %param.9) | copy-start | bytes 88
  7.2 1.8 %copy-start.1 = (bf16[7,96,1024]{2,1,0:T(8,128)(2,1)S(1)}, bf16[7,96,1024]{2,1,0:T(8,128)(2,1)}, u32[]{:S(2)}) copy-start(bf16[7,96,1024]{2,1,0:T(8,128)(2,1)} %param.8) | copy-start | bytes 4128772
  7.2 73.2 %all-gather.6.cloned.1.call-start = ((), (), s32[]{:S(2)}) async-start(), calls=%async_computation.1 | async-start | bytes 1474560 | tf_op jit(solution)/shard_map/all_gather | solution.py:96
  9.0 2.2 %copy-start.4 = (s32[512]{0:T(512)S(1)}, s32[512]{0:T(512)}, u32[]{:S(2)}) copy-start(s32[512]{0:T(512)} %param.10) | copy-start | bytes 6148
  17.7 20.2 %copy-start.5 = (f32[512]{0:T(512)S(1)}, f32[512]{0:T(512)}, u32[]{:S(2)}) copy-start(f32[512]{0:T(512)} %param.12) | copy-start | bytes 6148
  17.8 20.2 %copy-start.6 = (f32[512]{0:T(512)S(1)}, f32[512]{0:T(512)}, u32[]{:S(2)}) copy-start(f32[512]{0:T(512)} %param.11) | copy-start | bytes 6148
  17.8 34.8 %copy-start.3 = (f32[96,512]{1,0:T(8,128)S(1)}, f32[96,512]{1,0:T(8,128)}, u32[]{:S(2)}) copy-start(f32[96,512]{1,0:T(8,128)} %param.13) | copy-start | bytes 589828
  52.7 7.6 %collective-permute-start.1 = (bf16[192,512]{1,0:T(8,128)(2,1)S(1)}, bf16[192,512]{1,0:T(8,128)(2,1)S(1)}, u32[]{:S(2)}, u32[]{:S(2)}) collective-permute-start(bf16[192,512]{1,0:T(8,128)(2,1)S(1)} %pad_maximum_fusion.1), channel_id=1, source_target_pairs={{8,0},{16,8},{24,16},{9,1},{17,9},{25,17},{10,2},{18,10},{26,18},{... | collective-permute-start | bytes 589832 | tf_op jit(solution)/shard_map/ppermute | solution.py:18
  54.0 7.7 %collective-permute-start = (bf16[192,512]{1,0:T(8,128)(2,1)S(1)}, bf16[192,512]{1,0:T(8,128)(2,1)S(1)}, u32[]{:S(2)}, u32[]{:S(2)}) collective-permute-start(bf16[192,512]{1,0:T(8,128)(2,1)S(1)} %pad_maximum_fusion.1), channel_id=1, source_target_pairs={{0,8},{8,16},{16,24},{1,9},{9,17},{17,25},{2,10},{10,18},{18,26},{... | collective-permute-start | bytes 589832 | tf_op jit(solution)/shard_map/ppermute | solution.py:17
  62.5 62.0 %all-gather.4.cloned.1.call-start = ((), (), s32[]{:S(2)}) async-start(), calls=%async_computation | async-start | bytes 6881280 | tf_op jit(solution)/shard_map/all_gather | solution.py:95
  64.1 6.3 %collective-permute-start.3 = (f32[2,512]{1,0:T(2,128)S(1)}, f32[2,512]{1,0:T(2,128)S(1)}, u32[]{:S(2)}, u32[]{:S(2)}) collective-permute-start(f32[2,512]{1,0:T(2,128)S(1)} %pad_maximum_fusion.3), channel_id=1, source_target_pairs={{8,0},{16,8},{24,16},{9,1},{17,9},{25,17},{10,2},{18,10},{26,18},{... | collective-permute-start | bytes 12296 | tf_op jit(solution)/shard_map/ppermute | solution.py:18
  65.4 6.3 %collective-permute-start.2 = (f32[2,512]{1,0:T(2,128)S(1)}, f32[2,512]{1,0:T(2,128)S(1)}, u32[]{:S(2)}, u32[]{:S(2)}) collective-permute-start(f32[2,512]{1,0:T(2,128)S(1)} %pad_maximum_fusion.3), channel_id=1, source_target_pairs={{0,8},{8,16},{16,24},{1,9},{9,17},{17,25},{2,10},{10,18},{18,26},{... | collective-permute-start | bytes 12296 | tf_op jit(solution)/shard_map/ppermute | solution.py:17
  159.6 1.1 copy-start.2
Sparse Core Ops, SparseCore 0:
  62.6 17.7 all-gather.5
  82.6 41.8 all-gather.3
